TPU v7x, 32 devices: a whole 2x2x4 slice. The times are simulated.
32 devices in a mesh: section: 4 (over y, x), row: 8 (over z, core).
Axes of the slice: x: 2, y: 2, z: 4, core: 2. Of those that a mesh axis runs over, the one named last changes fastest.
Arguments:
- omega: bfloat16 [2048, 8192], P('section', 'row'), may hold values from -0.5 to 0.5
- basis: bfloat16 [8192, 1024], P('row', 'section'), may hold values from -6 to 6
- vectors: bfloat16 [4, 8192], P(None, 'row'), may hold values from -6 to 6
Outputs:
- ortho: float32 [4, 8192], P(None, ('row', 'section'))
- coeffs: float32 [4, 1024], P(None, 'section')
All inputs are finite; a program needn't handle non-finite values.
Results may differ from a plain program's by a relative error of at most 0.0021.
Values may be sent and summed in bfloat16 or wider, within the bound.
A program may use at most 64 MiB of HBM per device.

v0:
```python
import jax
import jax.numpy as jnp
from jax import lax
from jax.sharding import PartitionSpec as P


def from_behind(value, axis, steps):
    count = lax.axis_size(axis)
    initial, last = (max(0, -steps), min(count, count - steps))
    return lax.ppermute(value, axis, [(source, source + steps) for source in range(initial, last)])


def from_root(value, axis, source):
    kept = jnp.where(lax.axis_index(axis) == source, value, 0).astype(value.dtype)
    return lax.psum(kept, axis)


def lower_solve(factor, right):
    return lax.linalg.triangular_solve(factor, right, left_side=True, lower=True, transpose_a=False)


def factor_solve(factor, right):
    half = lower_solve(factor, right)
    return lax.linalg.triangular_solve(factor, half, left_side=True, lower=True, transpose_a=True)


def body(omega, basis, vectors):
    hi = lax.Precision.HIGHEST
    sections = lax.axis_size("section")
    my_section = lax.axis_index("section")
    whole = lax.all_gather(omega, "section", axis=0, tiled=True)
    sketch = lax.psum_scatter(
        jnp.dot(whole, basis, preferred_element_type=jnp.float32),
        "row",
        scatter_dimension=0,
        tiled=True,
    )
    probe_term = lax.dot_general(
        vectors, whole, (((1,), (1,)), ((), ())), preferred_element_type=jnp.float32
    )
    probe = lax.psum_scatter(probe_term, "row", scatter_dimension=1, tiled=True)
    gram = lax.psum(jnp.dot(sketch.T, sketch, precision=hi), "row")
    factor = jnp.linalg.cholesky(gram)

    def project(current):
        inner = jnp.dot(current, sketch, precision=hi)
        inner = lax.psum(inner, "row")
        coef = factor_solve(factor, inner.T).T
        return (coef, current - jnp.dot(coef, sketch.T, precision=hi))

    def advance(step, carry):
        current, kept = carry
        coef, moved = project(current)
        active = my_section == step
        kept = jnp.where(active, coef, kept)
        moved = jnp.where(active, moved, current)
        return (from_behind(moved, "section", 1), kept)

    start_coef = jnp.zeros((vectors.shape[0], basis.shape[1]), jnp.float32)
    probe, kept = lax.fori_loop(0, sections - 1, advance, (probe, start_coef))
    coef, moved = project(probe)
    finished = my_section == sections - 1
    kept = jnp.where(finished, coef, kept)
    final = from_root(moved, "section", sections - 1)
    rounded = kept.astype(jnp.bfloat16)
    own_term = lax.dot_general(
        rounded, basis, (((1,), (1,)), ((), ())), preferred_element_type=jnp.float32
    )
    removed = lax.psum_scatter(own_term, "section", scatter_dimension=1, tiled=True)
    width = removed.shape[1]
    mine = lax.dynamic_slice_in_dim(vectors, my_section * width, width, 1)
    remain = mine.astype(jnp.float32) - removed
    small = lax.psum(jnp.dot(final, final.T, precision=hi), "row")
    lower = jnp.linalg.cholesky(small)
    ortho = lower_solve(lower, remain)
    return (ortho, kept)


def solution(mesh):
    return jax.shard_map(
        body,
        mesh=mesh,
        in_specs=(P("section", "row"), P("row", "section"), P(None, "row")),
        out_specs=(P(None, ("row", "section")), P(None, "section")),
        check_vma=False,
    )
```

profile of v0, /device:TPU:0, one launch (start us, length us, event | category | flops | bytes accessed | tf_op | source)
XLA Modules:
  0.0 442.4 jit_solution(2750653464107480190)
XLA Ops:
  7.2 0.7 all-gather.2.cloned.1.call-update
  8.0 57.2 %all-gather.2.cloned.1.call-done = bf16[2048,1024]{1,0:T(8,128)(2,1)} async-done(((bf16[512,1024]{1,0:T(8,128)(2,1)}), bf16[2048,1024]{1,0:T(8,128)(2,1)}) %all-gather.2.cloned.1.call-update) | async-done | bytes 4194320 | tf_op jit(solution)/shard_map/all_gather | solution.py:31
  65.2 4.8 %fusion.36 = f32[2048,256]{1,0:T(8,128)} fusion(bf16[2048,1024]{1,0:T(8,128)(2,1)} %all-gather.2.cloned.1.call-done, bf16[1024,256]{1,0:T(8,128)(2,1)S(1)} %copy-done), kind=kOutput, calls=%fused_computation.78 | convolution fusion | flops 1073741824 | bytes 6815744 | tf_op jit(solution)/shard_map/dot_general | solution.py:33
  70.0 4.4 convolution_bitcast_fusion
  74.5 31.6 %reduce-scatter.8.cloned.1.call-done = f32[256,256]{1,0:T(8,128)} async-done(((f32[2048,256]{1,0:T(8,128)}), f32[256,256]{1,0:T(8,128)}) %reduce-scatter.8.cloned.1.call-update) | async-done | bytes 262160 | tf_op jit(solution)/shard_map/reduce_scatter | solution.py:32
  106.1 2.4 fusion.37
  108.8 30.9 %reduce-scatter.10.cloned.1.call-done = f32[256,4]{1,0:T(8,128)} async-done(((f32[2048,4]{1,0:T(8,128)}), f32[256,4]{1,0:T(8,128)}) %reduce-scatter.10.cloned.1.call-update) | async-done | bytes 4112
  139.7 1.0 copy.18
  140.7 54.8 %all-reduce.3.cloned.1.call-done = f32[256,256]{0,1:T(8,128)} async-done(((f32[256,256]{0,1:T(8,128)}), f32[256,256]{0,1:T(8,128)}) %all-reduce.3.cloned.1.call-update) | async-done | bytes 262160 | tf_op jit(solution)/shard_map/psum | solution.py:42
  195.5 1.1 copy.11
  196.6 1.0 fusion.11
  197.6 11.7 %cholesky.64 = f32[128,128]{1,0:T(8,128)S(1)} custom-call(f32[128,128]{1,0:T(8,128)S(1)} %cholesky.153), custom_call_target="Cholesky" | custom-call | tf_op jit(solution)/shard_map/jit(cholesky)/cholesky | solution.py:43
  209.4 9.8 %custom-call.23 = f32[1,128,128]{1,2,0:T(8,128)S(1)} custom-call(f32[1,128,128]{2,1,0:T(8,128)S(1)} %get-tuple-element.206), custom_call_target="InvertDiagBlocksLowerTriangular" | custom-call | tf_op jit(solution)/shard_map/jit(cholesky)/cholesky | solution.py:43
  219.7 11.7 %cholesky.131 = f32[128,128]{1,0:T(8,128)S(1)} custom-call(f32[128,128]{1,0:T(8,128)S(1)} %convolution_subtract_fusion.3), custom_call_target="Cholesky" | custom-call | tf_op jit(solution)/shard_map/jit(cholesky)/cholesky | solution.py:43
  231.4 0.7 compare_reduce_fusion.1
  233.5 4.2 while.27
  234.4 1.3 bitcast_dynamic-update-slice_fusion.4
  236.4 1.3 bitcast_dynamic-update-slice_fusion.4
  237.8 19.7 %custom-call.31 = f32[2,128,128]{1,2,0:T(8,128)S(1)} custom-call(f32[2,128,128]{2,1,0:T(8,128)S(1)} %get-tuple-element.168), custom_call_target="InvertDiagBlocksLowerTriangular" | custom-call | tf_op jit(solution)/shard_map/triangular_solve/custom-call.4 | solution.py:24
  257.4 133.4 %while.26 = (s32[]{:T(128)}, f32[4,256]{1,0:T(4,128)S(1)}, f32[4,256]{1,0:T(4,128)S(1)}, s32[]{:T(128)}, f32[256,256]{1,0:T(8,128)S(1)}, /*index=5*/f32[256,256]{1,0:T(8,128)S(1)}, s32[]{:T(128)}, s32[]{:T(128)}, s32[]{:T(128)}) while((s32[]{:T(128)}, f32[4,256]{1,0:T(4,128)S(1)}, f32[4,256]{1,0:T(4,128)S(1)}, s32[]{:T(128)}, ...), condition=%wide.region_9.12_spmd.clone, body=%wide.region_7.0_spmd.clone.sunk | while | flops 11149320 | bytes 1659231 | solution.py:60
  257.6 4.1 while.28
  258.3 1.3 bitcast_dynamic-update-slice_fusion.5
  260.3 1.3 bitcast_dynamic-update-slice_fusion.5
  261.6 19.7 %custom-call.37 = f32[2,128,128]{1,2,0:T(8,128)S(1)} custom-call(f32[2,128,128]{2,1,0:T(8,128)S(1)} %get-tuple-element.303), custom_call_target="InvertDiagBlocksLowerTriangular" | custom-call | tf_op jit(solution)/shard_map/while/body/eval_jaxpr/triangular_solve/custom-call.4 | solution.py:24
  281.5 13.7 %psum.45 = f32[256,4]{0,1:T(4,128)S(1)} all-reduce(f32[256,4]{0,1:T(4,128)S(1)} %fusion.99), channel_id=1, replica_groups=mesh['section'=4,'row'=8] {'row'}, use_global_device_ids=true, to_apply=%region_8.8 | all-reduce | flops 1024 | bytes 8192 | tf_op jit(solution)/shard_map/while/body/eval_jaxpr/psum | solution.py:47
  296.7 3.4 collective-permute-start
  300.1 1.3 collective-permute-done
  301.5 4.1 while.28
  302.2 1.3 bitcast_dynamic-update-slice_fusion.5
  304.2 1.3 bitcast_dynamic-update-slice_fusion.5
  305.6 19.7 %custom-call.37 = f32[2,128,128]{1,2,0:T(8,128)S(1)} custom-call(f32[2,128,128]{2,1,0:T(8,128)S(1)} %get-tuple-element.303), custom_call_target="InvertDiagBlocksLowerTriangular" | custom-call | tf_op jit(solution)/shard_map/while/body/eval_jaxpr/triangular_solve/custom-call.4 | solution.py:24
  325.5 13.6 %psum.45 = f32[256,4]{0,1:T(4,128)S(1)} all-reduce(f32[256,4]{0,1:T(4,128)S(1)} %fusion.99), channel_id=1, replica_groups=mesh['section'=4,'row'=8] {'row'}, use_global_device_ids=true, to_apply=%region_8.8 | all-reduce | flops 1024 | bytes 8192 | tf_op jit(solution)/shard_map/while/body/eval_jaxpr/psum | solution.py:47
  340.6 4.2 collective-permute-start
  344.8 1.3 collective-permute-done
  346.2 4.1 while.28
  346.2 0.7 fusion.106
  346.9 1.3 bitcast_dynamic-update-slice_fusion.5
  348.9 1.3 bitcast_dynamic-update-slice_fusion.5
  350.3 19.7 %custom-call.37 = f32[2,128,128]{1,2,0:T(8,128)S(1)} custom-call(f32[2,128,128]{2,1,0:T(8,128)S(1)} %get-tuple-element.303), custom_call_target="InvertDiagBlocksLowerTriangular" | custom-call | tf_op jit(solution)/shard_map/while/body/eval_jaxpr/triangular_solve/custom-call.4 | solution.py:24
  370.2 13.6 %psum.45 = f32[256,4]{0,1:T(4,128)S(1)} all-reduce(f32[256,4]{0,1:T(4,128)S(1)} %fusion.99), channel_id=1, replica_groups=mesh['section'=4,'row'=8] {'row'}, use_global_device_ids=true, to_apply=%region_8.8 | all-reduce | flops 1024 | bytes 8192 | tf_op jit(solution)/shard_map/while/body/eval_jaxpr/psum | solution.py:47
  385.2 4.3 collective-permute-start
  389.6 1.3 collective-permute-done
  391.1 13.6 %psum.40 = f32[256,4]{0,1:T(4,128)S(1)} all-reduce(f32[256,4]{0,1:T(4,128)S(1)} %fusion.38), channel_id=1, replica_groups=mesh['section'=4,'row'=8] {'row'}, use_global_device_ids=true, to_apply=%region_10.13 | all-reduce | flops 1024 | bytes 8192 | tf_op jit(solution)/shard_map/psum | solution.py:47
  405.9 1.0 convolution_bitcast_fusion.1
  407.2 11.0 %psum.41 = f32[4,256]{1,0:T(4,128)S(1)} all-reduce(f32[4,256]{1,0:T(4,128)S(1)} %fusion.10), channel_id=1, replica_groups=mesh['section'=4,'row'=8] {'section'}, use_global_device_ids=true, to_apply=%region_11.14 | all-reduce | flops 1024 | bytes 8192 | tf_op jit(solution)/shard_map/psum | solution.py:15
  418.3 13.6 %psum.42 = f32[4,4]{0,1:T(4,128)S(1)} all-reduce(f32[4,4]{0,1:T(4,128)S(1)} %fusion.39), channel_id=1, replica_groups=mesh['section'=4,'row'=8] {'row'}, use_global_device_ids=true, to_apply=%region_12.15 | all-reduce | flops 16 | bytes 128 | tf_op jit(solution)/shard_map/psum | solution.py:73
  434.1 1.0 copy.20
  435.0 0.8 fusion.22
  (100 shorter events, 15.1 us)
Async XLA Ops:
  7.2 58.0 %copy-start = (bf16[1024,256]{1,0:T(8,128)(2,1)S(1)}, bf16[1024,256]{1,0:T(8,128)(2,1)}, u32[]{:S(2)}) copy-start(bf16[1024,256]{1,0:T(8,128)(2,1)} %param.10) | copy-start | bytes 1572868
  7.2 58.0 %all-gather.2.cloned.1.call-start = ((), (), s32[]{:S(2)}) async-start(), calls=%async_computation.3 | async-start | bytes 5242880 | tf_op jit(solution)/shard_map/all_gather | solution.py:31
  7.9 62.1 %copy-start.3 = (bf16[4,1024]{1,0:T(4,128)(2,1)S(1)}, bf16[4,1024]{1,0:T(4,128)(2,1)}, u32[]{:S(2)}) copy-start(bf16[4,1024]{1,0:T(4,128)(2,1)} %param.11) | copy-start | bytes 24580
  7.9 98.2 %reduce-scatter.8.cloned.1.call-start = ((), (), s32[]{:S(2)}) async-start(), calls=%async_computation.4 | async-start | bytes 2359296 | tf_op jit(solution)/shard_map/reduce_scatter | solution.py:32
  70.0 69.7 %reduce-scatter.10.cloned.1.call-start = ((), (), s32[]{:S(2)}) async-start(), calls=%async_computation.6 | async-start | bytes 1179648
  74.5 121.0 %all-reduce.3.cloned.1.call-start = ((), (), s32[]{:S(2)}) async-start(), calls=%async_computation.5 | async-start | bytes 524288 | tf_op jit(solution)/shard_map/psum | solution.py:42
  106.1 151.3 %copy-start.1 = (f32[256,256]{1,0:T(8,128)S(1)}, f32[256,256]{1,0:T(8,128)}, u32[]{:S(2)}) copy-start(f32[256,256]{1,0:T(8,128)} %reduce-scatter.8.cloned.1.call-done) | copy-start | bytes 786436
  108.5 325.5 %reduce-scatter.12.cloned.1.call-start = ((), (), s32[]{:S(2)}) async-start(), calls=%async_computation.7 | async-start | bytes 655360
  296.7 4.7 %collective-permute-start = (f32[4,256]{1,0:T(4,128)S(1)}, f32[4,256]{1,0:T(4,128)S(1)}, u32[]{:S(2)}, u32[]{:S(2)}) collective-permute-start(f32[4,256]{1,0:T(4,128)S(1)} %fusion.104), channel_id=1, source_target_pairs={{0,8},{8,16},{16,24},{1,9},{9,17},{17,25},{2,10},{10,18},{18,26},{... | collective-permute-start | bytes 12296 | tf_op jit(solution)/shard_map/while/body/eval_jaxpr/ppermute | solution.py:10
  340.6 5.6 %collective-permute-start = (f32[4,256]{1,0:T(4,128)S(1)}, f32[4,256]{1,0:T(4,128)S(1)}, u32[]{:S(2)}, u32[]{:S(2)}) collective-permute-start(f32[4,256]{1,0:T(4,128)S(1)} %fusion.104), channel_id=1, source_target_pairs={{0,8},{8,16},{16,24},{1,9},{9,17},{17,25},{2,10},{10,18},{18,26},{... | collective-permute-start | bytes 12296 | tf_op jit(solution)/shard_map/while/body/eval_jaxpr/ppermute | solution.py:10
  385.2 5.6 %collective-permute-start = (f32[4,256]{1,0:T(4,128)S(1)}, f32[4,256]{1,0:T(4,128)S(1)}, u32[]{:S(2)}, u32[]{:S(2)}) collective-permute-start(f32[4,256]{1,0:T(4,128)S(1)} %fusion.104), channel_id=1, source_target_pairs={{0,8},{8,16},{16,24},{1,9},{9,17},{17,25},{2,10},{10,18},{18,26},{... | collective-permute-start | bytes 12296 | tf_op jit(solution)/shard_map/while/body/eval_jaxpr/ppermute | solution.py:10
  405.9 30.0 %copy-start.2 = (f32[4,256]{1,0:T(4,128)}, f32[4,256]{1,0:T(4,128)S(1)}, u32[]{:S(2)}) copy-start(f32[4,256]{1,0:T(4,128)S(1)} %bitcast_select_fusion.1) | copy-start | bytes 12292
Sparse Core Ops, SparseCore 0:
  9.8 55.2 all-gather.1
  70.1 35.9 reduce-scatter.7
  108.4 31.2 reduce-scatter.9
  141.9 53.5 all-reduce.2
  407.1 25.7 reduce-scatter.11
where the time goes:
time: 443 us; the launch traced here: 442 us
  waiting for transfers between devices  179 us (40%)
  other arithmetic  116 us (26%)
  blocking collectives  79.1 us (18%)
  matrix products  20.6 us (5%)
  local copies, waits for them, and re-layouts  19.6 us (4%)
  between operations  15.2 us (3%)
  starting transfers between devices  12.4 us (3%)
    another operation x16, other arithmetic, factor_solve(): lax.linalg.triangular_solve(factor, half, left_side=True, lower=True, tra...  78.8 us
    all_gather x1, waiting for transfers between devices, body(): whole = lax.all_gather(omega, 'section', axis=0, tiled=True)  57.2 us
    psum x1, waiting for transfers between devices, body(): gram = lax.psum(jnp.dot(sketch.T, sketch, precision=hi), 'row')  54.8 us
    psum x4, blocking collectives, project(): inner = lax.psum(inner, 'row')  54.5 us
    another operation x6, other arithmetic, body(): factor = jnp.linalg.cholesky(gram)  34 us
    unnamed x7, waiting for transfers between devices  31.7 us
    reduce_scatter x1, waiting for transfers between devices, body(): lax.psum_scatter(jnp.dot(whole, basis, preferred_element_type=jnp.float32...  31.6 us
    another operation x28, local copies, waits for them, and re-layouts, factor_solve(): lax.linalg.triangular_solve(factor, half, left_side=True, lower=True, tra...  16.4 us
  transfers between devices with their start and end apart: 8, of which 7 were waited for; matrix products, arithmetic and copies ran while one was open for 2% of the time, Pallas kernels for 0%

commit v1 on v0

--- a/solution.py
+++ b/solution.py
@@ -28,7 +28,14 @@
     hi = lax.Precision.HIGHEST
     sections = lax.axis_size("section")
     my_section = lax.axis_index("section")
-    whole = lax.all_gather(omega, "section", axis=0, tiled=True)
+    ring = [omega]
+    for hop in range(3):
+        ring.append(lax.ppermute(ring[-1], "section", [(dev, (dev + 1) % 4) for dev in range(4)]))
+    whole = jnp.roll(
+        jnp.concatenate(ring[::-1], axis=0),
+        (lax.axis_index("section") + 1) * ring[0].shape[0],
+        axis=0,
+    )
     sketch = lax.psum_scatter(
         jnp.dot(whole, basis, preferred_element_type=jnp.float32),
         "row",

time: 443 us -> 478 us (1.079)
  waiting for transfers between devices: 179 us -> 194 us
  local copies, waits for them, and re-layouts: 19.6 us -> 30.9 us
    ppermute x0 -> x3, waiting for transfers between devices: none -> 73.6 us  [body(): lax.ppermute(ring[-1], 'section', [(dev, (dev + 1) % 4) for dev in range(...]
    all_gather x1 -> x0, waiting for transfers between devices: 57.2 us -> none  [body(): whole = lax.all_gather(omega, 'section', axis=0, tiled=True)]
    unnamed x10 -> x20, local copies, waits for them, and re-layouts: 2 us -> 13.2 us
    unnamed x7 -> x6, waiting for transfers between devices: 31.7 us -> 30.9 us
  transfers between devices with their start and end apart: 8 -> 10, of which waited for: 7 -> 9; matrix products, arithmetic and copies ran while one was open for 2% -> 2% of each run, Pallas kernels for 0% -> 0%
where the time goes in v1:
time: 478 us; the launch traced here: 477 us
  waiting for transfers between devices  194 us (41%)
  other arithmetic  116 us (24%)
  blocking collectives  79.1 us (17%)
  local copies, waits for them, and re-layouts  30.9 us (6%)
  matrix products  25.1 us (5%)
  starting transfers between devices  16.1 us (3%)
  between operations  15.2 us (3%)
    another operation x16, other arithmetic, factor_solve(): lax.linalg.triangular_solve(factor, half, left_side=True, lower=True, tra...  78.8 us
    ppermute x3, waiting for transfers between devices, body(): lax.ppermute(ring[-1], 'section', [(dev, (dev + 1) % 4) for dev in range(...  73.6 us
    psum x1, waiting for transfers between devices, body(): gram = lax.psum(jnp.dot(sketch.T, sketch, precision=hi), 'row')  54.9 us
    psum x4, blocking collectives, project(): inner = lax.psum(inner, 'row')  54.6 us
    another operation x6, other arithmetic, body(): factor = jnp.linalg.cholesky(gram)  34 us
    reduce_scatter x1, waiting for transfers between devices, body(): lax.psum_scatter(jnp.dot(whole, basis, preferred_element_type=jnp.float32...  31.2 us
    unnamed x6, waiting for transfers between devices  30.9 us
    another operation x28, local copies, waits for them, and re-layouts, factor_solve(): lax.linalg.triangular_solve(factor, half, left_side=True, lower=True, tra...  16.4 us
  transfers between devices with their start and end apart: 10, of which 9 were waited for; matrix products, arithmetic and copies ran while one was open for 2% of the time, Pallas kernels for 0%

profile of v1, /device:TPU:0, one launch (start us, length us, event | category | flops | bytes accessed | tf_op | source)
XLA Modules:
  0.0 477.2 jit_solution(10943322785466974252)
XLA Ops:
  7.2 3.0 collective-permute-start.1
  10.3 24.3 %collective-permute-done.1 = bf16[512,1024]{1,0:T(8,128)(2,1)S(1)} collective-permute-done((bf16[512,1024]{1,0:T(8,128)(2,1)}, bf16[512,1024]{1,0:T(8,128)(2,1)S(1)}, u32[]{:S(2)}, u32[]{:S(2)}) %collective-permute-start.1) | collective-permute-done | bytes 1048608 | tf_op jit(solution)/shard_map/ppermute | solution.py:33
  35.4 24.5 %collective-permute-done.2 = bf16[512,1024]{1,0:T(8,128)(2,1)} collective-permute-done((bf16[512,1024]{1,0:T(8,128)(2,1)S(1)}, bf16[512,1024]{1,0:T(8,128)(2,1)}, u32[]{:S(2)}, u32[]{:S(2)}) %collective-permute-start.2) | collective-permute-done | bytes 1048608 | tf_op jit(solution)/shard_map/ppermute | solution.py:33
  59.9 24.7 %collective-permute-done.3 = bf16[512,1024]{1,0:T(8,128)(2,1)} collective-permute-done((bf16[512,1024]{1,0:T(8,128)(2,1)}, bf16[512,1024]{1,0:T(8,128)(2,1)}, u32[]{:S(2)}, u32[]{:S(2)}) %collective-permute-start.3) | collective-permute-done | bytes 1048608 | tf_op jit(solution)/shard_map/ppermute | solution.py:33
  84.6 1.3 constant_dynamic-update-slice_fusion.7
  85.9 1.3 constant_dynamic-update-slice_fusion.6
  87.3 1.3 constant_dynamic-update-slice_fusion.4
  88.6 1.3 constant_dynamic-update-slice_fusion.3
  89.9 1.3 constant_dynamic-update-slice_fusion.2
  91.4 3.2 copy-done.2
  94.6 2.7 fusion.10
  97.3 3.4 fusion.14
  100.7 1.4 copy.17
  102.2 31.2 %reduce-scatter.8.cloned.1.call-done = f32[256,256]{1,0:T(8,128)} async-done(((f32[2048,256]{1,0:T(8,128)}), f32[256,256]{1,0:T(8,128)}) %reduce-scatter.8.cloned.1.call-update) | async-done | bytes 262160 | tf_op jit(solution)/shard_map/reduce_scatter | solution.py:39
  133.3 2.3 fusion.45
  135.9 30.9 %reduce-scatter.10.cloned.1.call-done = f32[256,4]{1,0:T(8,128)} async-done(((f32[2048,4]{1,0:T(8,128)}), f32[256,4]{1,0:T(8,128)}) %reduce-scatter.10.cloned.1.call-update) | async-done | bytes 4112
  167.8 54.9 %all-reduce.3.cloned.1.call-done = f32[256,256]{0,1:T(8,128)} async-done(((f32[256,256]{0,1:T(8,128)}), f32[256,256]{0,1:T(8,128)}) %all-reduce.3.cloned.1.call-update) | async-done | bytes 262160 | tf_op jit(solution)/shard_map/psum | solution.py:49
  224.8 11.7 %cholesky.64 = f32[128,128]{1,0:T(8,128)S(1)} custom-call(f32[128,128]{1,0:T(8,128)S(1)} %cholesky.153), custom_call_target="Cholesky" | custom-call | tf_op jit(solution)/shard_map/jit(cholesky)/cholesky | solution.py:50
  236.6 9.8 %custom-call.23 = f32[1,128,128]{1,2,0:T(8,128)S(1)} custom-call(f32[1,128,128]{2,1,0:T(8,128)S(1)} %get-tuple-element.206), custom_call_target="InvertDiagBlocksLowerTriangular" | custom-call | tf_op jit(solution)/shard_map/jit(cholesky)/cholesky | solution.py:50
  246.9 11.7 %cholesky.131 = f32[128,128]{1,0:T(8,128)S(1)} custom-call(f32[128,128]{1,0:T(8,128)S(1)} %convolution_subtract_fusion.3), custom_call_target="Cholesky" | custom-call | tf_op jit(solution)/shard_map/jit(cholesky)/cholesky | solution.py:50
  260.7 4.2 while.27
  261.6 1.3 bitcast_dynamic-update-slice_fusion.4
  263.6 1.3 bitcast_dynamic-update-slice_fusion.4
  265.0 19.7 %custom-call.31 = f32[2,128,128]{1,2,0:T(8,128)S(1)} custom-call(f32[2,128,128]{2,1,0:T(8,128)S(1)} %get-tuple-element.168), custom_call_target="InvertDiagBlocksLowerTriangular" | custom-call | tf_op jit(solution)/shard_map/triangular_solve/custom-call.4 | solution.py:24
  284.7 139.1 %while.26 = (s32[]{:T(128)}, f32[4,256]{1,0:T(4,128)S(1)}, f32[4,256]{1,0:T(4,128)S(1)}, s32[]{:T(128)}, f32[256,256]{1,0:T(8,128)}, /*index=5*/f32[256,256]{1,0:T(8,128)S(1)}, s32[]{:T(128)}, s32[]{:T(128)}, s32[]{:T(128)}) while((s32[]{:T(128)}, f32[4,256]{1,0:T(4,128)S(1)}, f32[4,256]{1,0:T(4,128)S(1)}, s32[]{:T(128)}, ...), condition=%wide.region_9.12_spmd.clone, body=%wide.region_7.11_spmd.clone.sunk | while | flops 11149320 | bytes 1659231 | solution.py:67
  284.8 4.1 while.28
  285.5 1.3 bitcast_dynamic-update-slice_fusion.5
  287.5 1.3 bitcast_dynamic-update-slice_fusion.5
  288.9 19.7 %custom-call.39 = f32[2,128,128]{1,2,0:T(8,128)S(1)} custom-call(f32[2,128,128]{2,1,0:T(8,128)S(1)} %get-tuple-element.303), custom_call_target="InvertDiagBlocksLowerTriangular" | custom-call | tf_op jit(solution)/shard_map/while/body/eval_jaxpr/triangular_solve/custom-call.4 | solution.py:24
  309.7 13.7 %psum.45 = f32[256,4]{0,1:T(4,128)S(1)} all-reduce(f32[256,4]{0,1:T(4,128)S(1)} %fusion.105), channel_id=1, replica_groups=mesh['section'=4,'row'=8] {'row'}, use_global_device_ids=true, to_apply=%region_8.8 | all-reduce | flops 1024 | bytes 8192 | tf_op jit(solution)/shard_map/while/body/eval_jaxpr/psum | solution.py:54
  325.8 3.4 collective-permute-start
  329.3 1.3 collective-permute-done
  330.6 4.1 while.28
  331.3 1.3 bitcast_dynamic-update-slice_fusion.5
  333.4 1.3 bitcast_dynamic-update-slice_fusion.5
  334.7 19.7 %custom-call.39 = f32[2,128,128]{1,2,0:T(8,128)S(1)} custom-call(f32[2,128,128]{2,1,0:T(8,128)S(1)} %get-tuple-element.303), custom_call_target="InvertDiagBlocksLowerTriangular" | custom-call | tf_op jit(solution)/shard_map/while/body/eval_jaxpr/triangular_solve/custom-call.4 | solution.py:24
  355.6 13.6 %psum.45 = f32[256,4]{0,1:T(4,128)S(1)} all-reduce(f32[256,4]{0,1:T(4,128)S(1)} %fusion.105), channel_id=1, replica_groups=mesh['section'=4,'row'=8] {'row'}, use_global_device_ids=true, to_apply=%region_8.8 | all-reduce | flops 1024 | bytes 8192 | tf_op jit(solution)/shard_map/while/body/eval_jaxpr/psum | solution.py:54
  371.6 4.2 collective-permute-start
  375.8 1.3 collective-permute-done
  377.2 4.1 while.28
  377.9 1.3 bitcast_dynamic-update-slice_fusion.5
  379.9 1.3 bitcast_dynamic-update-slice_fusion.5
  381.3 19.7 %custom-call.39 = f32[2,128,128]{1,2,0:T(8,128)S(1)} custom-call(f32[2,128,128]{2,1,0:T(8,128)S(1)} %get-tuple-element.303), custom_call_target="InvertDiagBlocksLowerTriangular" | custom-call | tf_op jit(solution)/shard_map/while/body/eval_jaxpr/triangular_solve/custom-call.4 | solution.py:24
  402.1 13.6 %psum.45 = f32[256,4]{0,1:T(4,128)S(1)} all-reduce(f32[256,4]{0,1:T(4,128)S(1)} %fusion.105), channel_id=1, replica_groups=mesh['section'=4,'row'=8] {'row'}, use_global_device_ids=true, to_apply=%region_8.8 | all-reduce | flops 1024 | bytes 8192 | tf_op jit(solution)/shard_map/while/body/eval_jaxpr/psum | solution.py:54
  418.2 4.3 collective-permute-start
  425.0 13.6 %psum.40 = f32[256,4]{0,1:T(4,128)S(1)} all-reduce(f32[256,4]{0,1:T(4,128)S(1)} %fusion.46), channel_id=1, replica_groups=mesh['section'=4,'row'=8] {'row'}, use_global_device_ids=true, to_apply=%region_10.13 | all-reduce | flops 1024 | bytes 8192 | tf_op jit(solution)/shard_map/psum | solution.py:54
  442.1 11.0 %psum.41 = f32[4,256]{1,0:T(4,128)S(1)} all-reduce(f32[4,256]{1,0:T(4,128)S(1)} %fusion.17), channel_id=1, replica_groups=mesh['section'=4,'row'=8] {'section'}, use_global_device_ids=true, to_apply=%region_11.14 | all-reduce | flops 1024 | bytes 8192 | tf_op jit(solution)/shard_map/psum | solution.py:15
  453.2 13.6 %psum.42 = f32[4,4]{0,1:T(4,128)S(1)} all-reduce(f32[4,4]{0,1:T(4,128)S(1)} %fusion.47), channel_id=1, replica_groups=mesh['section'=4,'row'=8] {'row'}, use_global_device_ids=true, to_apply=%region_12.15 | all-reduce | flops 16 | bytes 128 | tf_op jit(solution)/shard_map/psum | solution.py:80
  (114 shorter events, 32.2 us)
Async XLA Ops:
  7.2 87.4 %copy-start = (bf16[1024,256]{1,0:T(8,128)(2,1)S(1)}, bf16[1024,256]{1,0:T(8,128)(2,1)}, u32[]{:S(2)}) copy-start(bf16[1024,256]{1,0:T(8,128)(2,1)} %param.10) | copy-start | bytes 1572868
  7.2 84.1 %copy-start.1 = (bf16[512,1024]{1,0:T(8,128)(2,1)S(1)}, bf16[512,1024]{1,0:T(8,128)(2,1)}, u32[]{:S(2)}) copy-start(bf16[512,1024]{1,0:T(8,128)(2,1)} %param.9) | copy-start | bytes 3145732
  7.2 126.1 %reduce-scatter.8.cloned.1.call-start = ((), (), s32[]{:S(2)}) async-start(), calls=%async_computation.3 | async-start | bytes 2359296 | tf_op jit(solution)/shard_map/reduce_scatter | solution.py:39
  7.2 27.3 %collective-permute-start.1 = (bf16[512,1024]{1,0:T(8,128)(2,1)}, bf16[512,1024]{1,0:T(8,128)(2,1)S(1)}, u32[]{:S(2)}, u32[]{:S(2)}) collective-permute-start(bf16[512,1024]{1,0:T(8,128)(2,1)} %param.9), channel_id=1, source_target_pairs={{0,8},{8,16},{16,24},{24,0},{1,9},{9,17},{17,25},{25,1},{2,10},{10... | collective-permute-start | bytes 3145736 | tf_op jit(solution)/shard_map/ppermute | solution.py:33
  34.6 25.3 %collective-permute-start.2 = (bf16[512,1024]{1,0:T(8,128)(2,1)S(1)}, bf16[512,1024]{1,0:T(8,128)(2,1)}, u32[]{:S(2)}, u32[]{:S(2)}) collective-permute-start(bf16[512,1024]{1,0:T(8,128)(2,1)S(1)} %collective-permute-done.1), channel_id=1, source_target_pairs={{0,8},{8,16},{16,24},{24,0},{1,9},{9,17},{17,25},{25,1},{2,10},{10... | collective-permute-start | bytes 3145736 | tf_op jit(solution)/shard_map/ppermute | solution.py:33
  59.9 24.7 %collective-permute-start.3 = (bf16[512,1024]{1,0:T(8,128)(2,1)}, bf16[512,1024]{1,0:T(8,128)(2,1)}, u32[]{:S(2)}, u32[]{:S(2)}) collective-permute-start(bf16[512,1024]{1,0:T(8,128)(2,1)} %collective-permute-done.2), channel_id=1, source_target_pairs={{0,8},{8,16},{16,24},{24,0},{1,9},{9,17},{17,25},{25,1},{2,10},{10... | collective-permute-start | bytes 3145736 | tf_op jit(solution)/shard_map/ppermute | solution.py:33
  91.2 6.2 %copy-start.4 = (bf16[4,1024]{1,0:T(4,128)(2,1)S(1)}, bf16[4,1024]{1,0:T(4,128)(2,1)}, u32[]{:S(2)}) copy-start(bf16[4,1024]{1,0:T(4,128)(2,1)} %param.11) | copy-start | bytes 24580
  91.3 3.2 copy-start.2
  97.3 69.5 %reduce-scatter.10.cloned.1.call-start = ((), (), s32[]{:S(2)}) async-start(), calls=%async_computation.5 | async-start | bytes 1179648
  102.1 120.6 %all-reduce.3.cloned.1.call-start = ((), (), s32[]{:S(2)}) async-start(), calls=%async_computation.4 | async-start | bytes 524288 | tf_op jit(solution)/shard_map/psum | solution.py:49
  135.7 333.2 %reduce-scatter.12.cloned.1.call-start = ((), (), s32[]{:S(2)}) async-start(), calls=%async_computation.6 | async-start | bytes 655360
  325.8 4.7 collective-permute-start
  371.6 5.5 %collective-permute-start = (f32[4,256]{1,0:T(4,128)S(1)}, f32[4,256]{1,0:T(4,128)S(1)}, u32[]{:S(2)}, u32[]{:S(2)}) collective-permute-start(f32[4,256]{1,0:T(4,128)S(1)} %fusion.110), channel_id=1, source_target_pairs={{0,8},{8,16},{16,24},{1,9},{9,17},{17,25},{2,10},{10,18},{18,26},{... | collective-permute-start | bytes 12296 | tf_op jit(solution)/shard_map/while/body/eval_jaxpr/ppermute | solution.py:10
  418.2 5.6 %collective-permute-start = (f32[4,256]{1,0:T(4,128)S(1)}, f32[4,256]{1,0:T(4,128)S(1)}, u32[]{:S(2)}, u32[]{:S(2)}) collective-permute-start(f32[4,256]{1,0:T(4,128)S(1)} %fusion.110), channel_id=1, source_target_pairs={{0,8},{8,16},{16,24},{1,9},{9,17},{17,25},{2,10},{10,18},{18,26},{... | collective-permute-start | bytes 12296 | tf_op jit(solution)/shard_map/while/body/eval_jaxpr/ppermute | solution.py:10
  439.7 31.0 %copy-start.3 = (f32[4,256]{1,0:T(4,128)}, f32[4,256]{1,0:T(4,128)S(1)}, u32[]{:S(2)}) copy-start(f32[4,256]{1,0:T(4,128)S(1)} %bitcast_select_fusion.1) | copy-start | bytes 12292
Sparse Core Ops, SparseCore 0:
  97.4 35.8 reduce-scatter.7
  135.6 31.1 reduce-scatter.9
  169.1 53.5 all-reduce.2
  441.0 25.7 reduce-scatter.11
